TPU v7x, 32 devices: a whole 2x2x4 slice. The times are simulated.
32 devices in a mesh: row: 8 (over z, x), col: 4 (over y, core).
Axes of the slice: x: 2, y: 2, z: 4, core: 2. Of those that a mesh axis runs over, the one named last changes fastest.
Arguments:
- rhs: bfloat16 [2, 4096, 2048], P(None, 'row', 'col'), may hold values from -6 to 6
- panel: bfloat16 [2, 4096, 1024], P(None, 'row', 'col'), may hold values from -0.25 to 0.25
- pivots: float32 [1024], P('col'), may hold values from 2 to 4
Outputs:
- updated: float32 [2, 4096, 2048], P(None, 'row', 'col')
All inputs are finite; a program needn't handle non-finite values.
Results may differ from a plain program's by a relative error of at most 0.0045.
Values may be sent and summed in bfloat16 or wider, within the bound.
A program may use at most 64 MiB of HBM per device.

v0:
```python
import jax
import jax.numpy as jnp
from jax import lax
from jax.sharding import PartitionSpec as P


def spread(block, axis, owner):
    block = jnp.where(lax.axis_index(axis) == owner, block, jnp.zeros_like(block))
    return lax.psum(block, axis)


def lower_solve(matrix, values):
    return lax.linalg.triangular_solve(matrix, values, left_side=True, lower=True)


def diagonal_tile(tile_rows, pivots_all, step):
    width = tile_rows.shape[0]
    strict = jnp.tril(tile_rows[:, step * width : (step + 1) * width].astype(jnp.float32), -1)
    return strict + jnp.diag(pivots_all[step * width : (step + 1) * width])


def on_device(rhs, panel, pivots):
    layers = rhs.shape[0]
    width = rhs.shape[1]
    columns = rhs.shape[2]
    row_index = lax.axis_index("row")
    whole, pivots_all = (
        lax.all_gather(panel, "col", axis=2, tiled=True),
        lax.all_gather(pivots.astype(jnp.bfloat16), "col", axis=0, tiled=True).astype(pivots.dtype),
    )
    left = whole.reshape(layers * width, 2 * width)
    received = []
    for step in range(2):
        received.append((spread(rhs[0], "row", step), spread(whole[0], "row", step)))
    first = lower_solve(
        diagonal_tile(received[0][1], pivots_all, 0), received[0][0].astype(jnp.float32)
    )
    first_low = first.astype(jnp.bfloat16)
    second_side = received[1][0].astype(jnp.float32) - jnp.dot(
        received[1][1][:, 0:width], first_low, preferred_element_type=jnp.float32
    )
    second = lower_solve(diagonal_tile(received[1][1], pivots_all, 1), second_side)
    second_low = second.astype(jnp.bfloat16)
    both_low = jnp.concatenate([first_low, second_low], axis=0)
    product = jnp.dot(left, both_low, preferred_element_type=jnp.float32).reshape(
        layers, width, columns
    )
    current = rhs.astype(jnp.float32) - product
    head = jnp.where(row_index == 0, first, jnp.where(row_index == 1, second, current[0]))
    return current.at[0].set(head)


def solution(mesh):
    placed = (P(None, "row", "col"), P(None, "row", "col"), P("col"))
    return jax.shard_map(
        on_device, mesh=mesh, in_specs=placed, out_specs=P(None, "row", "col"), check_vma=False
    )
```

profile of v0, /device:TPU:28, one launch (start us, length us, event | category | flops | bytes accessed | tf_op | source)
XLA Modules:
  0.0 291.7 jit_solution(7297288299672975428)
XLA Ops:
  7.3 2.1 select_bitcast_fusion.2
  9.4 22.4 %all-gather.3.cloned.1.call-done = bf16[2,512,1024]{2,1,0:T(8,128)(2,1)} async-done(((bf16[2,512,256]{2,1,0:T(8,128)(2,1)}), bf16[2,512,1024]{2,1,0:T(8,128)(2,1)}) %all-gather.3.cloned.1.call-update) | async-done | bytes 2097168 | tf_op jit(solution)/shard_map/all_gather | solution.py:28
  31.7 2.7 select_bitcast_fusion
  35.1 5.1 %all-gather = bf16[4,1,256]{2,1,0:T(2,128)(2,1)S(1)} all-gather(bf16[1,1,256]{2,1,0:T(2,128)(2,1)S(1)} %reshape.94), channel_id=1, replica_groups=mesh['row'=8,'col'=4] {'col'}, dimensions={0}, use_global_device_ids=true | all-gather | bytes 2560 | tf_op jit(solution)/shard_map/all_gather | solution.py:29
  40.2 123.2 %all-reduce.3.cloned.1.call-done = (bf16[512,512]{1,0:T(8,128)(2,1)}, bf16[512,1024]{1,0:T(8,128)(2,1)}, bf16[512,512]{1,0:T(8,128)(2,1)}, bf16[512,1024]{1,0:T(8,128)(2,1)}) async-done(((bf16[512,512]{1,0:T(8,128)(2,1)}, bf16[512,1024]{1,0:T(8,128)(2,1)}, bf16[512,512]{1,0:T(8,128)(2,1)}, bf16[512,1024]{1,0:T(8,128)(2,1)}), (bf16[512,512]{1,0:T(8,128)(2,1)}, bf16[512,1024]{1,0:T(8,128)(2,1)}, ...) | async-done | bytes 3145744 | tf_op jit(solution)/shard_map/psum | solution.py:9
  163.4 1.6 fusion.7
  165.1 8.5 %while.5 = (s32[]{:T(128)}, f32[512,512]{1,0:T(8,128)S(1)}, s32[4,2]{0,1:T(2,128)S(1)}, f32[4,128,128]{2,1,0:T(8,128)S(1)}, s32[]{:T(128)}) while((s32[]{:T(128)}, f32[512,512]{1,0:T(8,128)S(1)}, s32[4,2]{0,1:T(2,128)S(1)}, f32[4,128,128]{2,1,0:T(8,128)S(1)}, s32[]{:T(128)}) %tuple.43), condition=%wide.while_cond.1, body=%wide.while_body.1.sunk | while | flops 2 | bytes 131181 | solution.py:13
  165.8 1.4 bitcast_dynamic-update-slice_fusion.4
  167.9 1.4 bitcast_dynamic-update-slice_fusion.4
  170.0 1.4 bitcast_dynamic-update-slice_fusion.4
  172.1 1.4 bitcast_dynamic-update-slice_fusion.4
  173.6 39.3 %custom-call.4 = f32[4,128,128]{1,2,0:T(8,128)S(1)} custom-call(f32[4,128,128]{2,1,0:T(8,128)S(1)} %get-tuple-element.32), custom_call_target="InvertDiagBlocksLowerTriangular" | custom-call | tf_op jit(solution)/shard_map/triangular_solve/custom-call.1 | solution.py:13
  217.3 8.4 %while.6 = (s32[]{:T(128)}, f32[512,512]{1,0:T(8,128)S(1)}, s32[4,2]{0,1:T(2,128)S(1)}, f32[4,128,128]{2,1,0:T(8,128)S(1)}, s32[]{:T(128)}) while((s32[]{:T(128)}, f32[512,512]{1,0:T(8,128)S(1)}, s32[4,2]{0,1:T(2,128)S(1)}, f32[4,128,128]{2,1,0:T(8,128)S(1)}, s32[]{:T(128)}) %tuple.54), condition=%wide.while_cond.1.clone, body=%wide.while_body.1.clone.sunk | while | flops 2 | bytes 131181 | solution.py:13
  217.9 1.4 bitcast_dynamic-update-slice_fusion.5
  220.0 1.4 bitcast_dynamic-update-slice_fusion.5
  222.1 1.4 bitcast_dynamic-update-slice_fusion.5
  224.2 1.4 bitcast_dynamic-update-slice_fusion.5
  226.3 40.1 %custom-call.5 = f32[4,128,128]{1,2,0:T(8,128)S(1)} custom-call(f32[4,128,128]{2,1,0:T(8,128)} %copy-done.11), custom_call_target="InvertDiagBlocksLowerTriangular" | custom-call | tf_op jit(solution)/shard_map/triangular_solve/custom-call.1 | solution.py:13
  266.5 1.6 convolution_subtract_fusion
  270.6 1.4 fusion.37
  274.7 2.6 convolution_bitcast_fusion
  277.4 1.9 copy.5
  279.3 3.0 %convert_subtract_fusion = f32[2,512,512]{2,1,0:T(8,128)} fusion(f32[2,512,512]{2,1,0:T(8,128)S(1)} %bitcast.82, bf16[2,512,512]{2,1,0:T(8,128)(2,1)} %param.7), kind=kLoop, calls=%fused_computation.4 | loop fusion | flops 1048576 | bytes 5242880 | tf_op jit(solution)/shard_map/sub | solution.py:48
  282.3 2.6 fusion.3
  (70 shorter events, 16.9 us)
Async XLA Ops:
  6.5 25.2 %all-gather.3.cloned.1.call-start = ((), (), s32[]{:S(2)}) async-start(), calls=%async_computation | async-start | bytes 2621440 | tf_op jit(solution)/shard_map/all_gather | solution.py:28
  7.3 156.1 %all-reduce.3.cloned.1.call-start = ((), (), s32[]{:S(2)}) async-start(), calls=%async_computation.1 | async-start | bytes 6291456 | tf_op jit(solution)/shard_map/psum | solution.py:9
  34.5 0.7 copy-start.12
  163.4 49.5 %copy-start.7 = (bf16[512,512]{1,0:T(8,128)(2,1)S(1)}, bf16[512,512]{1,0:T(8,128)(2,1)}, u32[]{:S(2)}) copy-start(bf16[512,512]{1,0:T(8,128)(2,1)} %get-tuple-element.50) | copy-start | bytes 1572868
  212.9 1.8 copy-start.10
  215.8 50.7 %copy-start.6 = (bf16[512,512]{1,0:T(8,128)(2,1)S(1)}, bf16[512,512]{1,0:T(8,128)(2,1)}, u32[]{:S(2)}) copy-start(bf16[512,512]{1,0:T(8,128)(2,1)} %get-tuple-element.52) | copy-start | bytes 1572868
  217.1 49.3 %copy-start.2 = (f32[128,512]{1,0:T(8,128)}, f32[128,512]{1,0:T(8,128)S(1)}, u32[]{:S(2)}) copy-start(f32[128,512]{1,0:T(8,128)S(1)} %fusion.40) | copy-start | bytes 786436
  225.6 0.7 copy-start.11
  266.5 2.0 copy-start.9
  270.6 4.1 %copy-start.8 = (bf16[2,512,1024]{2,1,0:T(8,128)(2,1)S(1)}, bf16[2,512,1024]{2,1,0:T(8,128)(2,1)}, u32[]{:S(2)}) copy-start(bf16[2,512,1024]{2,1,0:T(8,128)(2,1)} %all-gather.3.cloned.1.call-done) | copy-start | bytes 6291460
  272.0 2.7 copy-start
  273.9 0.7 copy-start.4
  279.3 3.0 %copy-start.1 = (f32[128,512]{1,0:T(8,128)S(1)}, f32[128,512]{1,0:T(8,128)}, u32[]{:S(2)}) copy-start(f32[128,512]{1,0:T(8,128)} %copy-done) | copy-start | bytes 786436
  279.3 3.0 %copy-start.3 = (f32[128,512]{1,0:T(8,128)S(1)}, f32[128,512]{1,0:T(8,128)}, u32[]{:S(2)}) copy-start(f32[128,512]{1,0:T(8,128)} %copy-done.2) | copy-start | bytes 786436
  279.3 3.0 %copy-start.5 = (f32[128,512]{1,0:T(8,128)S(1)}, f32[128,512]{1,0:T(8,128)}, u32[]{:S(2)}) copy-start(f32[128,512]{1,0:T(8,128)} %copy-done.4) | copy-start | bytes 786436
Sparse Core Ops, SparseCore 0:
  8.9 22.8 all-gather.2
  35.6 127.7 all-reduce.2
where the time goes:
time: 296 us; the launch traced here: 292 us
  waiting for transfers between devices  146 us (49%)
  other arithmetic  91.7 us (31%)
  local copies, waits for them, and re-layouts  20.7 us (7%)
  matrix products  14 us (5%)
  between operations  13.8 us (5%)
  blocking collectives  5.05 us (2%)
    psum x1, waiting for transfers between devices, spread(): return lax.psum(block, axis)  123 us
    another operation x4, other arithmetic, lower_solve(): lax.linalg.triangular_solve(matrix, values, left_side=True, lower=True)  81.1 us
    all_gather x1, waiting for transfers between devices, on_device(): lax.all_gather(panel, 'col', axis=2, tiled=True)  22.4 us
    another operation x27, local copies, waits for them, and re-layouts, lower_solve(): lax.linalg.triangular_solve(matrix, values, left_side=True, lower=True)  16.7 us
    another operation x14, matrix products, lower_solve(): lax.linalg.triangular_solve(matrix, values, left_side=True, lower=True)  9.78 us
  transfers between devices with their start and end apart: 2, of which 2 were waited for; matrix products, arithmetic and copies ran while one was open for 1% of the time, Pallas kernels for 0%

commit v1 on v0

v1 whole, which is shorter than its diff:
```python
import functools

import jax
import jax.numpy as jnp
from jax import lax
from jax.experimental import pallas as pl
from jax.experimental.pallas import tpu as pltpu
from jax.sharding import PartitionSpec as P

MESH = pl.DeviceIdType.MESH
LANES = 128
PIECES = 2
HALVES = 2
F32 = jnp.float32
BF16 = jnp.bfloat16


def mm(a, b):
    return jnp.dot(a, b, preferred_element_type=F32)


def mm32(a, b):
    return jnp.dot(a, b, preferred_element_type=F32, precision=lax.Precision.HIGHEST)


def split(a):
    high = a.astype(BF16)
    return high, (a - high.astype(F32)).astype(BF16)


def unit_inverse(n):
    size = n.shape[0]
    if size > LANES:
        half = size // 2
        top = unit_inverse(n[:half, :half])
        low = unit_inverse(n[half:, half:])
        corner = -mm32(low, mm32(n[half:, :half], top))
        return jnp.concatenate(
            [
                jnp.concatenate([top, jnp.zeros((half, half), F32)], axis=1),
                jnp.concatenate([corner, low], axis=1),
            ],
            axis=0,
        )
    row = lax.broadcasted_iota(jnp.int32, (size, size), 0)
    col = lax.broadcasted_iota(jnp.int32, (size, size), 1)
    base = 4
    small = jnp.where((row >> base) == (col >> base), n, 0.0)
    total = jnp.where(row == col, 1.0, 0.0) - small
    power = small
    for _ in range(base - 1):
        power = mm32(power, power)
        total = total + mm32(total, power)
    shift = base
    while (1 << shift) < size:
        inside = ((row >> (shift + 1)) == (col >> (shift + 1))) & (
            (row >> shift) != (col >> shift)
        )
        total = total - mm32(total, mm32(jnp.where(inside, n, 0.0), total))
        shift += 1
    return total


def kernel(
    rows,
    cols,
    rhs,
    panel,
    pivots,
    out,
    gat,
    piv,
    xl,
    low_tri,
    inv_hi,
    inv_lo,
    scale,
    g_send,
    g_recv,
    f_send,
    p_send,
    p_recv,
    z_send,
    x_send,
    x_recv,
):
    r = lax.axis_index("row")
    c = lax.axis_index("col")
    line = lax.rem(r, 2)
    depth = r // 2
    depths = rows // 2
    layers, width, columns = rhs.shape
    cw = panel.shape[2]
    half = cols // 2
    ys = cols // 2
    y, core = c // 2, lax.rem(c, 2)
    chunks = columns // LANES
    piece_rows = width // PIECES
    part_rows = width // HALVES
    partner = y * 2 + 1 - core

    barrier = pltpu.get_barrier_semaphore()
    for d in range(1, cols):
        pl.semaphore_signal(
            barrier, inc=1, device_id={"col": lax.rem(c + d, cols)}, device_id_type=MESH
        )
    pl.semaphore_signal(
        barrier, inc=1, device_id={"row": depth * 2 + 1 - line}, device_id_type=MESH
    )

    @pl.when(depth > 0)
    def _():
        pl.semaphore_signal(barrier, inc=1, device_id={"row": r - 2}, device_id_type=MESH)

    @pl.when(depth < depths - 1)
    def _():
        pl.semaphore_signal(barrier, inc=1, device_id={"row": r + 2}, device_id_type=MESH)

    peers = cols + jnp.where(depth > 0, 1, 0) + jnp.where(depth < depths - 1, 1, 0)
    pl.semaphore_wait(barrier, peers)

    def own(k, t, h):
        part = pl.ds(h * part_rows, part_rows)
        target = partner if k == 0 else lax.rem(y + k, ys) * 2 + core
        return pltpu.make_async_remote_copy(
            src_ref=panel.at[t, part],
            dst_ref=gat.at[c, t, part],
            send_sem=g_send.at[k, t, h],
            recv_sem=g_recv.at[c, t, h],
            device_id={"col": target},
            device_id_type=MESH,
        )

    def relay(k, t, h):
        part = pl.ds(h * part_rows, part_rows)
        source = lax.rem(y + ys - k, ys) * 2 + core
        return pltpu.make_async_remote_copy(
            src_ref=gat.at[source, t, part],
            dst_ref=gat.at[source, t, part],
            send_sem=f_send.at[k, t, h],
            recv_sem=g_recv.at[source, t, h],
            device_id={"col": partner},
            device_id_type=MESH,
        )

    def arrived(source, t, h):
        part = pl.ds(h * part_rows, part_rows)
        pltpu.make_async_remote_copy(
            src_ref=gat.at[source, t, part],
            dst_ref=gat.at[source, t, part],
            send_sem=f_send.at[0, t, h],
            recv_sem=g_recv.at[source, t, h],
            device_id={"col": partner},
            device_id_type=MESH,
        ).wait_recv()

    def pivot_copy(d, source):
        return pltpu.make_async_remote_copy(
            src_ref=pivots,
            dst_ref=piv.at[source],
            send_sem=p_send.at[d],
            recv_sem=p_recv.at[source],
            device_id={"col": lax.rem(c + d, cols)},
            device_id_type=MESH,
        )

    @pl.when(depth == 0)
    def _():
        for d in range(1, cols):
            pivot_copy(d, c).start()

    for t in range(layers):
        for h in range(HALVES):
            for k in range(ys):
                own(k, t, h).start()
    gat[c] = panel[...]

    def take_layer(t):
        for h in range(HALVES):
            for k in range(1, ys):
                source = lax.rem(y + ys - k, ys) * 2 + core
                arrived(source, t, h)
                relay(k, t, h).start()
        for h in range(HALVES):
            for k in range(ys):
                arrived(lax.rem(y + ys - k, ys) * 2 + 1 - core, t, h)

    take_layer(0)

    def piece(s, n, q):
        return xl.at[s, n, pl.ds(q * piece_rows, piece_rows)]

    def down(s, n, q):
        return pltpu.make_async_remote_copy(
            src_ref=piece(s, n, q),
            dst_ref=piece(s, n, q),
            send_sem=z_send.at[n, q],
            recv_sem=x_recv.at[s, n, q],
            device_id={"row": r + 2},
            device_id_type=MESH,
        )

    def across(s, n, q):
        return pltpu.make_async_remote_copy(
            src_ref=piece(s, n, q),
            dst_ref=piece(s, n, q),
            send_sem=x_send.at[n, q],
            recv_sem=x_recv.at[s, n, q],
            device_id={"row": depth * 2 + 1 - line},
            device_id_type=MESH,
        )

    def forward(n, q):
        across(line, n, q).start()

        @pl.when(depth < depths - 1)
        def _():
            down(line, n, q).start()

    def lanes(n):
        return pl.ds(pl.multiple_of(n * LANES, LANES), LANES)

    def product(s, t, n):
        total = None
        for j in range(half):
            term = mm(gat[s * half + j, t], xl[s, n, pl.ds(j * cw, cw)])
            total = term if total is None else total + term
        return total

    @pl.when(depth == 0)
    def _():
        for d in range(1, cols):
            pivot_copy(d, lax.rem(c + d, cols)).wait_recv()
        piv[c] = pivots[...]
        for j in range(half):
            low_tri[:, j * cw : (j + 1) * cw] = gat[line * half + j, 0]
        recip = 1.0 / jnp.concatenate([piv[line * half + j] for j in range(half)], axis=1)
        row = lax.broadcasted_iota(jnp.int32, (width, width), 0)
        col = lax.broadcasted_iota(jnp.int32, (width, width), 1)
        scaled = jnp.where(row > col, low_tri[...].astype(F32) * recip, 0.0)
        scale[...] = jnp.broadcast_to(
            jnp.sum(jnp.where(row == col, recip, 0.0), axis=1, keepdims=True), scale.shape
        )
        high, low = split(unit_inverse(scaled))
        inv_hi[...] = high
        inv_lo[...] = low

    @pl.when(r == 0)
    def _():
        @pl.loop(0, chunks)
        def _(n):
            side = rhs[0, :, lanes(n)]
            x = (mm(inv_hi[...], side) + mm(inv_lo[...], side)) * scale[...]
            xl[0, n] = x.astype(BF16)
            out[0, :, lanes(n)] = x
            for q in range(PIECES):
                forward(n, q)

    @pl.when(r == 1)
    def _():
        @pl.loop(0, chunks)
        def _(n):
            for q in range(PIECES):
                across(0, n, q).wait_recv()
            side = rhs[0, :, lanes(n)].astype(F32) - product(0, 0, n)
            high, low = split(side)
            x = (mm(inv_hi[...], high) + mm(inv_lo[...], high) + mm(inv_hi[...], low)) * scale[...]
            xl[1, n] = x.astype(BF16)
            out[0, :, lanes(n)] = x
            for q in range(PIECES):
                forward(n, q)

    for t in range(1, layers):
        take_layer(t)

    @pl.loop(0, chunks)
    def _(n):
        @pl.when(depth > 0)
        def _():
            for q in range(PIECES):
                across(line, n, q).wait_recv()
                forward(n, q)
            out[0, :, lanes(n)] = rhs[0, :, lanes(n)].astype(F32) - product(line, 0, n)

        for t in range(1, layers):
            out[t, :, lanes(n)] = rhs[t, :, lanes(n)].astype(F32) - product(line, t, n)

    other = 1 - line

    @pl.loop(0, chunks)
    def _(n):
        @pl.when(r != 1)
        def _():
            for q in range(PIECES):
                across(other, n, q).wait_recv()

        @pl.when(depth > 0)
        def _():
            out[0, :, lanes(n)] -= product(other, 0, n)

        for t in range(1, layers):
            out[t, :, lanes(n)] -= product(other, t, n)

    for t in range(layers):
        for h in range(HALVES):
            for k in range(ys):
                own(k, t, h).wait_send()
            for k in range(1, ys):
                relay(k, t, h).wait_send()

    @pl.when(depth == 0)
    def _():
        for d in range(1, cols):
            pivot_copy(d, c).wait_send()

    @pl.loop(0, chunks)
    def _(n):
        for q in range(PIECES):
            across(line, n, q).wait_send()

            @pl.when(depth < depths - 1)
            def _():
                down(line, n, q).wait_send()


def on_device(rows, cols, rhs, panel, pivots):
    layers, width, columns = rhs.shape
    cw = panel.shape[2]
    pw = pivots.shape[0]
    ys = cols // 2
    chunks = columns // LANES
    dma = pltpu.SemaphoreType.DMA
    vmem = pl.BlockSpec(memory_space=pltpu.VMEM)
    return pl.pallas_call(
        functools.partial(kernel, rows, cols),
        out_shape=jax.ShapeDtypeStruct((layers, width, columns), F32),
        in_specs=[vmem] * 3,
        out_specs=vmem,
        scratch_shapes=[
            pltpu.VMEM((cols, layers, width, cw), BF16),
            pltpu.VMEM((cols, 1, pw), F32),
            pltpu.VMEM((2, chunks, width, LANES), BF16),
            pltpu.VMEM((width, width), BF16),
            pltpu.VMEM((width, width), BF16),
            pltpu.VMEM((width, width), BF16),
            pltpu.VMEM((width, LANES), F32),
            dma((ys, layers, HALVES)),
            dma((cols, layers, HALVES)),
            dma((ys, layers, HALVES)),
            dma((cols,)),
            dma((cols,)),
            dma((chunks, PIECES)),
            dma((chunks, PIECES)),
            dma((2, chunks, PIECES)),
        ],
        compiler_params=pltpu.CompilerParams(
            collective_id=0, has_side_effects=True, vmem_limit_bytes=56 * 1024 * 1024
        ),
        name="solve_and_update",
    )(rhs, panel, pivots.reshape(1, pw))


def solution(mesh):
    placed = (P(None, "row", "col"), P(None, "row", "col"), P("col"))
    return jax.shard_map(
        functools.partial(on_device, mesh.shape["row"], mesh.shape["col"]),
        mesh=mesh,
        in_specs=placed,
        out_specs=P(None, "row", "col"),
        check_vma=False,
    )
```

time: 296 us -> 55.4 us (0.19)
  the two profiles are of different devices: /device:TPU:28 before, /device:TPU:24 now
where the time goes in v1:
time: 55.4 us; the launch traced here: 55.2 us
  Pallas kernels  52.1 us (94%)
  local copies, waits for them, and re-layouts  3.08 us (6%)
    pallas_call x1, Pallas kernels, on_device(): pl.pallas_call(functools.partial(kernel, rows, cols), out_shape=jax.Shape...  52.1 us
    unnamed x1, local copies, waits for them, and re-layouts  3.08 us

profile of v1, /device:TPU:24, one launch (start us, length us, event | category | flops | bytes accessed | tf_op | source)
XLA Modules:
  0.0 55.2 jit_solution(3678805440237371042)
XLA Ops:
  0.0 52.1 %solve_and_update.1 = f32[2,512,512]{2,1,0:T(8,128)} custom-call(bf16[2,512,512]{2,1,0:T(8,128)(2,1)} %rhs.1, bf16[2,512,256]{2,1,0:T(8,128)(2,1)} %panel.1, f32[1,256]{1,0:T(1,128)} %bitcast.1), custom_call_target="tpu_custom_call" | custom-call | tf_op jit(solution)/shard_map/solve_and_update/pallas_call | solution.py:334
  52.1 3.1 %copy.5 = f32[2,512,512]{2,1,0:T(8,128)} copy(f32[2,512,512]{2,1,0:T(8,128)} %solve_and_update.1) | data formatting | bytes 4194304

commit v2 on v1

--- a/solution.py
+++ b/solution.py
@@ -19,54 +19,59 @@
     return jnp.dot(a, b, preferred_element_type=F32)
 
 
-def mm32(a, b):
-    return jnp.dot(a, b, preferred_element_type=F32, precision=lax.Precision.HIGHEST)
-
-
 def split(a):
     high = a.astype(BF16)
     return high, (a - high.astype(F32)).astype(BF16)
 
 
+def mm3(a, b):
+    ah, al = split(a)
+    bh, bl = split(b)
+    return mm(ah, bh) + (mm(ah, bl) + mm(al, bh))
+
+
 def unit_inverse(n):
-    size = n.shape[0]
-    if size > LANES:
-        half = size // 2
-        top = unit_inverse(n[:half, :half])
-        low = unit_inverse(n[half:, half:])
-        corner = -mm32(low, mm32(n[half:, :half], top))
-        return jnp.concatenate(
-            [
-                jnp.concatenate([top, jnp.zeros((half, half), F32)], axis=1),
-                jnp.concatenate([corner, low], axis=1),
-            ],
-            axis=0,
-        )
-    row = lax.broadcasted_iota(jnp.int32, (size, size), 0)
-    col = lax.broadcasted_iota(jnp.int32, (size, size), 1)
+    width = n.shape[0]
+    row = lax.broadcasted_iota(jnp.int32, (LANES, LANES), 0)
+    col = lax.broadcasted_iota(jnp.int32, (LANES, LANES), 1)
     base = 4
-    small = jnp.where((row >> base) == (col >> base), n, 0.0)
-    total = jnp.where(row == col, 1.0, 0.0) - small
-    power = small
+    blocks = [n[i : i + LANES, i : i + LANES] for i in range(0, width, LANES)]
+    power = [jnp.where((row >> base) == (col >> base), b, 0.0) for b in blocks]
+    done = [jnp.where(row == col, 1.0, 0.0) - p for p in power]
     for _ in range(base - 1):
-        power = mm32(power, power)
-        total = total + mm32(total, power)
+        power = [mm3(p, p) for p in power]
+        done = [d + mm3(d, p) for d, p in zip(done, power)]
     shift = base
-    while (1 << shift) < size:
+    while (1 << shift) < LANES:
         inside = ((row >> (shift + 1)) == (col >> (shift + 1))) & (
             (row >> shift) != (col >> shift)
         )
-        total = total - mm32(total, mm32(jnp.where(inside, n, 0.0), total))
+        right = [mm3(jnp.where(inside, b, 0.0), d) for b, d in zip(blocks, done)]
+        done = [d - mm3(d, m) for d, m in zip(done, right)]
         shift += 1
-    return total
+    size = LANES
+    while size < width:
+        pairs = []
+        for i in range(0, len(done), 2):
+            top, low, at = done[i], done[i + 1], i * size
+            corner = -mm3(low, mm3(n[at + size : at + 2 * size, at : at + size], top))
+            first = jnp.concatenate([top, jnp.zeros((size, size), F32)], axis=1)
+            pairs.append(
+                jnp.concatenate([first, jnp.concatenate([corner, low], axis=1)], axis=0)
+            )
+        done = pairs
+        size *= 2
+    return done[0]
 
 
 def kernel(
     rows,
     cols,
+    rhs_in,
+    panel_in,
+    pivots,
+    out_to,
     rhs,
-    panel,
-    pivots,
     out,
     gat,
     piv,
@@ -83,6 +88,8 @@
     z_send,
     x_send,
     x_recv,
+    in_sem,
+    out_sem,
 ):
     r = lax.axis_index("row")
     c = lax.axis_index("col")
@@ -90,7 +97,7 @@
     depth = r // 2
     depths = rows // 2
     layers, width, columns = rhs.shape
-    cw = panel.shape[2]
+    cw = panel_in.shape[2]
     half = cols // 2
     ys = cols // 2
     y, core = c // 2, lax.rem(c, 2)
@@ -99,6 +106,11 @@
     part_rows = width // HALVES
     partner = y * 2 + 1 - core
 
+    panel_copy = pltpu.make_async_copy(panel_in, gat.at[c], in_sem.at[0])
+    rhs_copy = pltpu.make_async_copy(rhs_in, rhs, in_sem.at[1])
+    panel_copy.start()
+    rhs_copy.start()
+
     barrier = pltpu.get_barrier_semaphore()
     for d in range(1, cols):
         pl.semaphore_signal(
@@ -123,7 +135,7 @@
         part = pl.ds(h * part_rows, part_rows)
         target = partner if k == 0 else lax.rem(y + k, ys) * 2 + core
         return pltpu.make_async_remote_copy(
-            src_ref=panel.at[t, part],
+            src_ref=gat.at[c, t, part],
             dst_ref=gat.at[c, t, part],
             send_sem=g_send.at[k, t, h],
             recv_sem=g_recv.at[c, t, h],
@@ -169,21 +181,36 @@
         for d in range(1, cols):
             pivot_copy(d, c).start()
 
+    def needed(source, t, h, do):
+        if t > 0:
+            do()
+            return
+        read = (source < half) & ((h + 1) * part_rows > source * cw)
+
+        @pl.when((r > 0) | read)
+        def _():
+            do()
+
+    panel_copy.wait()
     for t in range(layers):
         for h in range(HALVES):
-            for k in range(ys):
-                own(k, t, h).start()
-    gat[c] = panel[...]
+            for k in range(ys - 1, -1, -1):
+                needed(c, t, h, lambda: own(k, t, h).start())
 
     def take_layer(t):
         for h in range(HALVES):
             for k in range(1, ys):
                 source = lax.rem(y + ys - k, ys) * 2 + core
-                arrived(source, t, h)
-                relay(k, t, h).start()
+
+                def pass_on():
+                    arrived(source, t, h)
+                    relay(k, t, h).start()
+
+                needed(source, t, h, pass_on)
         for h in range(HALVES):
             for k in range(ys):
-                arrived(lax.rem(y + ys - k, ys) * 2 + 1 - core, t, h)
+                source = lax.rem(y + ys - k, ys) * 2 + 1 - core
+                needed(source, t, h, lambda: arrived(source, t, h))
 
     take_layer(0)
 
@@ -245,6 +272,8 @@
         inv_hi[...] = high
         inv_lo[...] = low
 
+    rhs_copy.wait()
+
     @pl.when(r == 0)
     def _():
         @pl.loop(0, chunks)
@@ -273,40 +302,65 @@
     for t in range(1, layers):
         take_layer(t)
 
-    @pl.loop(0, chunks)
-    def _(n):
-        @pl.when(depth > 0)
-        def _():
+    def leave(n):
+        return pltpu.make_async_copy(
+            out.at[:, :, lanes(n)], out_to.at[:, :, lanes(n)], out_sem.at[n]
+        )
+
+    def start(t, n):
+        return rhs[t, :, lanes(n)].astype(F32)
+
+    @pl.when(line == 0)
+    def _():
+        @pl.loop(0, chunks)
+        def _(n):
+            @pl.when(depth > 0)
+            def _():
+                for q in range(PIECES):
+                    across(0, n, q).wait_recv()
+                    forward(n, q)
+                out[0, :, lanes(n)] = start(0, n) - product(0, 0, n)
+
+            for t in range(1, layers):
+                out[t, :, lanes(n)] = start(t, n) - product(0, t, n)
+
+        @pl.loop(0, chunks)
+        def _(n):
             for q in range(PIECES):
-                across(line, n, q).wait_recv()
-                forward(n, q)
-            out[0, :, lanes(n)] = rhs[0, :, lanes(n)].astype(F32) - product(line, 0, n)
-
-        for t in range(1, layers):
-            out[t, :, lanes(n)] = rhs[t, :, lanes(n)].astype(F32) - product(line, t, n)
-
-    other = 1 - line
-
-    @pl.loop(0, chunks)
-    def _(n):
-        @pl.when(r != 1)
-        def _():
-            for q in range(PIECES):
-                across(other, n, q).wait_recv()
-
-        @pl.when(depth > 0)
-        def _():
-            out[0, :, lanes(n)] -= product(other, 0, n)
-
-        for t in range(1, layers):
-            out[t, :, lanes(n)] -= product(other, t, n)
+                across(1, n, q).wait_recv()
+
+            @pl.when(depth > 0)
+            def _():
+                out[0, :, lanes(n)] -= product(1, 0, n)
+
+            for t in range(1, layers):
+                out[t, :, lanes(n)] -= product(1, t, n)
+            leave(n).start()
+
+    @pl.when(line == 1)
+    def _():
+        @pl.loop(0, chunks)
+        def _(n):
+            @pl.when(depth > 0)
+            def _():
+                for q in range(PIECES):
+                    across(1, n, q).wait_recv()
+                    forward(n, q)
+                for q in range(PIECES):
+                    across(0, n, q).wait_recv()
+                out[0, :, lanes(n)] = start(0, n) - product(0, 0, n) - product(1, 0, n)
+
+            for t in range(1, layers):
+                out[t, :, lanes(n)] = start(t, n) - product(0, t, n) - product(1, t, n)
+            leave(n).start()
 
     for t in range(layers):
         for h in range(HALVES):
             for k in range(ys):
-                own(k, t, h).wait_send()
+                needed(c, t, h, lambda: own(k, t, h).wait_send())
             for k in range(1, ys):
-                relay(k, t, h).wait_send()
+                source = lax.rem(y + ys - k, ys) * 2 + core
+                needed(source, t, h, lambda: relay(k, t, h).wait_send())
 
     @pl.when(depth == 0)
     def _():
@@ -321,6 +375,8 @@
             @pl.when(depth < depths - 1)
             def _():
                 down(line, n, q).wait_send()
+
+        leave(n).wait()
 
 
 def on_device(rows, cols, rhs, panel, pivots):
@@ -331,12 +387,16 @@
     chunks = columns // LANES
     dma = pltpu.SemaphoreType.DMA
     vmem = pl.BlockSpec(memory_space=pltpu.VMEM)
+    anywhere = pl.BlockSpec(memory_space=pl.ANY)
+    far = pl.BlockSpec(memory_space=pltpu.HBM)
     return pl.pallas_call(
         functools.partial(kernel, rows, cols),
         out_shape=jax.ShapeDtypeStruct((layers, width, columns), F32),
-        in_specs=[vmem] * 3,
-        out_specs=vmem,
+        in_specs=[far, far, vmem],
+        out_specs=anywhere,
         scratch_shapes=[
+            pltpu.VMEM((layers, width, columns), BF16),
+            pltpu.VMEM((layers, width, columns), F32),
             pltpu.VMEM((cols, layers, width, cw), BF16),
             pltpu.VMEM((cols, 1, pw), F32),
             pltpu.VMEM((2, chunks, width, LANES), BF16),
@@ -352,9 +412,11 @@
             dma((chunks, PIECES)),
             dma((chunks, PIECES)),
             dma((2, chunks, PIECES)),
+            dma((2,)),
+            dma((chunks,)),
         ],
         compiler_params=pltpu.CompilerParams(
-            collective_id=0, has_side_effects=True, vmem_limit_bytes=56 * 1024 * 1024
+            collective_id=0, has_side_effects=True, vmem_limit_bytes=24 * 1024 * 1024
         ),
         name="solve_and_update",
     )(rhs, panel, pivots.reshape(1, pw))

time: 55.4 us -> 47.3 us (0.85)
  the two profiles are of different devices: /device:TPU:24 before, /device:TPU:28 now
where the time goes in v2:
time: 47.3 us; the launch traced here: 47.1 us
  Pallas kernels  42.8 us (90%)
  local copies, waits for them, and re-layouts  4.27 us (9%)
    pallas_call x1, Pallas kernels, on_device(): pl.pallas_call(functools.partial(kernel, rows, cols), out_shape=jax.Shape...  42.8 us
    unnamed x7, local copies, waits for them, and re-layouts  4.27 us

profile of v2, /device:TPU:28, one launch (start us, length us, event | category | flops | bytes accessed | tf_op | source)
XLA Modules:
  0.0 47.1 jit_solution(16933614657133921072)
XLA Ops:
  0.0 0.0 copy-start
  0.0 1.2 %copy-done = bf16[2,512,512]{2,1,0:T(8,128)(2,1)S(1)} copy-done((bf16[2,512,512]{2,1,0:T(8,128)(2,1)S(1)}, bf16[2,512,512]{2,1,0:T(8,128)(2,1)}, u32[]{:S(2)}) %copy-start) | copy-done | bytes 1048600
  1.2 0.0 copy-start.1
  1.2 1.0 %copy-done.1 = bf16[2,512,256]{2,1,0:T(8,128)(2,1)S(1)} copy-done((bf16[2,512,256]{2,1,0:T(8,128)(2,1)S(1)}, bf16[2,512,256]{2,1,0:T(8,128)(2,1)}, u32[]{:S(2)}) %copy-start.1) | copy-done | bytes 524312
  2.3 0.0 copy-start.2
  2.3 0.7 %copy-done.2 = f32[256]{0:T(256)S(1)} copy-done((f32[256]{0:T(256)S(1)}, f32[256]{0:T(256)}, u32[]{:S(2)}) %copy-start.2) | copy-done | bytes 1048
  2.9 42.8 %solve_and_update.1 = f32[2,512,512]{2,1,0:T(8,128)S(1)} custom-call(bf16[2,512,512]{2,1,0:T(8,128)(2,1)S(1)} %copy-done, bf16[2,512,256]{2,1,0:T(8,128)(2,1)S(1)} %copy-done.1, f32[1,256]{1,0:T(1,128)S(1)} %bitcast.1), custom_call_target="tpu_custom_call" | custom-call | tf_op jit(solution)/shard_map/solve_and_update/pallas_call | solution.py:392
  45.8 1.3 %copy.5 = f32[2,512,512]{2,1,0:T(8,128)} copy(f32[2,512,512]{2,1,0:T(8,128)S(1)} %solve_and_update.1) | data formatting | bytes 4194304
Async XLA Ops:
  0.0 1.2 %copy-start = (bf16[2,512,512]{2,1,0:T(8,128)(2,1)S(1)}, bf16[2,512,512]{2,1,0:T(8,128)(2,1)}, u32[]{:S(2)}) copy-start(bf16[2,512,512]{2,1,0:T(8,128)(2,1)} %rhs_in.1) | copy-start | bytes 3145732
  1.2 1.0 %copy-start.1 = (bf16[2,512,256]{2,1,0:T(8,128)(2,1)S(1)}, bf16[2,512,256]{2,1,0:T(8,128)(2,1)}, u32[]{:S(2)}) copy-start(bf16[2,512,256]{2,1,0:T(8,128)(2,1)} %panel_in.1) | copy-start | bytes 1572868
  2.3 0.7 %copy-start.2 = (f32[256]{0:T(256)S(1)}, f32[256]{0:T(256)}, u32[]{:S(2)}) copy-start(f32[256]{0:T(256)} %param.5) | copy-start | bytes 3076

commit v3 on v2

--- a/solution.py
+++ b/solution.py
@@ -9,8 +9,8 @@
 
 MESH = pl.DeviceIdType.MESH
 LANES = 128
-PIECES = 2
-HALVES = 2
+PIECES = 4
+HALVES = 4
 F32 = jnp.float32
 BF16 = jnp.bfloat16
 
@@ -30,12 +30,12 @@
     return mm(ah, bh) + (mm(ah, bl) + mm(al, bh))
 
 
-def unit_inverse(n):
-    width = n.shape[0]
+def unit_inverses(parts):
+    size, whole = LANES, parts[0].shape[0]
     row = lax.broadcasted_iota(jnp.int32, (LANES, LANES), 0)
     col = lax.broadcasted_iota(jnp.int32, (LANES, LANES), 1)
     base = 4
-    blocks = [n[i : i + LANES, i : i + LANES] for i in range(0, width, LANES)]
+    blocks = [n[i : i + LANES, i : i + LANES] for n in parts for i in range(0, whole, LANES)]
     power = [jnp.where((row >> base) == (col >> base), b, 0.0) for b in blocks]
     done = [jnp.where(row == col, 1.0, 0.0) - p for p in power]
     for _ in range(base - 1):
@@ -49,11 +49,12 @@
         right = [mm3(jnp.where(inside, b, 0.0), d) for b, d in zip(blocks, done)]
         done = [d - mm3(d, m) for d, m in zip(done, right)]
         shift += 1
-    size = LANES
-    while size < width:
+    while size < whole:
+        each = whole // (2 * size)
         pairs = []
         for i in range(0, len(done), 2):
-            top, low, at = done[i], done[i + 1], i * size
+            n, at = parts[i // 2 // each], (i // 2 % each) * 2 * size
+            top, low = done[i], done[i + 1]
             corner = -mm3(low, mm3(n[at + size : at + 2 * size, at : at + size], top))
             first = jnp.concatenate([top, jnp.zeros((size, size), F32)], axis=1)
             pairs.append(
@@ -61,7 +62,7 @@
             )
         done = pairs
         size *= 2
-    return done[0]
+    return done
 
 
 def kernel(
@@ -80,6 +81,7 @@
     inv_hi,
     inv_lo,
     scale,
+    ends,
     g_send,
     g_recv,
     f_send,
@@ -181,23 +183,22 @@
         for d in range(1, cols):
             pivot_copy(d, c).start()
 
-    def needed(source, t, h, do):
+    def below(source, h):
+        return h // (HALVES // 2) - source // (half // 2)
+
+    def when_needed(source, t, h, do):
         if t > 0:
             do()
-            return
-        read = (source < half) & ((h + 1) * part_rows > source * cw)
-
-        @pl.when((r > 0) | read)
-        def _():
-            do()
+        else:
+            pl.when((r > 0) | (below(source, h) >= 0))(do)
 
     panel_copy.wait()
     for t in range(layers):
         for h in range(HALVES):
             for k in range(ys - 1, -1, -1):
-                needed(c, t, h, lambda: own(k, t, h).start())
-
-    def take_layer(t):
+                when_needed(c, t, h, lambda: own(k, t, h).start())
+
+    def take(t, wanted):
         for h in range(HALVES):
             for k in range(1, ys):
                 source = lax.rem(y + ys - k, ys) * 2 + core
@@ -206,13 +207,14 @@
                     arrived(source, t, h)
                     relay(k, t, h).start()
 
-                needed(source, t, h, pass_on)
+                wanted(source, h, pass_on)
         for h in range(HALVES):
             for k in range(ys):
                 source = lax.rem(y + ys - k, ys) * 2 + 1 - core
-                needed(source, t, h, lambda: arrived(source, t, h))
-
-    take_layer(0)
+                wanted(source, h, lambda: arrived(source, t, h))
+
+    def every(source, h, do):
+        do()
 
     def piece(s, n, q):
         return xl.at[s, n, pl.ds(q * piece_rows, piece_rows)]
@@ -254,23 +256,70 @@
             total = term if total is None else total + term
         return total
 
-    @pl.when(depth == 0)
-    def _():
+    middle = width // 2
+
+    def tile_part(below_by, first):
+        for j in range(half):
+            at = (first + below_by) * middle
+            if j // (half // 2) == first:
+                low_tri[at : at + middle, j * cw : (j + 1) * cw] = gat[
+                    line * half + j, 0, at : at + middle
+                ]
+
+    def recip_of(first):
+        ps = [piv[line * half + first * (half // 2) + j] for j in range(half // 2)]
+        return 1.0 / (ps[0] if len(ps) == 1 else jnp.concatenate(ps, axis=1))
+
+    def keep(at, to, value):
+        high, low = split(value)
+        inv_hi[at : at + middle, to : to + middle] = high
+        inv_lo[at : at + middle, to : to + middle] = low
+
+    def diagonal_halves():
         for d in range(1, cols):
             pivot_copy(d, lax.rem(c + d, cols)).wait_recv()
         piv[c] = pivots[...]
-        for j in range(half):
-            low_tri[:, j * cw : (j + 1) * cw] = gat[line * half + j, 0]
-        recip = 1.0 / jnp.concatenate([piv[line * half + j] for j in range(half)], axis=1)
-        row = lax.broadcasted_iota(jnp.int32, (width, width), 0)
-        col = lax.broadcasted_iota(jnp.int32, (width, width), 1)
-        scaled = jnp.where(row > col, low_tri[...].astype(F32) * recip, 0.0)
-        scale[...] = jnp.broadcast_to(
-            jnp.sum(jnp.where(row == col, recip, 0.0), axis=1, keepdims=True), scale.shape
-        )
-        high, low = split(unit_inverse(scaled))
-        inv_hi[...] = high
-        inv_lo[...] = low
+        row = lax.broadcasted_iota(jnp.int32, (middle, middle), 0)
+        col = lax.broadcasted_iota(jnp.int32, (middle, middle), 1)
+        parts = []
+        for i in range(2):
+            tile_part(0, i)
+            at = i * middle
+            recip = recip_of(i)
+            here = low_tri[at : at + middle, at : at + middle].astype(F32)
+            parts.append(jnp.where(row > col, here * recip, 0.0))
+            scale[at : at + middle] = jnp.broadcast_to(
+                jnp.sum(jnp.where(row == col, recip, 0.0), axis=1, keepdims=True),
+                (middle, LANES),
+            )
+        for i, inverse in enumerate(unit_inverses(parts)):
+            ends[i] = inverse
+            keep(i * middle, i * middle, inverse)
+        keep(0, middle, jnp.zeros((middle, middle), F32))
+
+    def corner():
+        tile_part(1, 0)
+        here = low_tri[middle:, :middle].astype(F32) * recip_of(0)
+        keep(middle, 0, -mm3(ends[1], mm3(here, ends[0])))
+
+    @pl.when(r == 0)
+    def _():
+        take(0, lambda source, h, do: pl.when(below(source, h) == 0)(do))
+        diagonal_halves()
+        take(
+            0,
+            lambda source, h, do: pl.when((source < half) & (below(source, h) > 0))(do),
+        )
+        corner()
+
+    @pl.when(r > 0)
+    def _():
+        take(0, every)
+
+    @pl.when(r == 1)
+    def _():
+        diagonal_halves()
+        corner()
 
     rhs_copy.wait()
 
@@ -300,7 +349,7 @@
                 forward(n, q)
 
     for t in range(1, layers):
-        take_layer(t)
+        take(t, every)
 
     def leave(n):
         return pltpu.make_async_copy(
@@ -357,10 +406,10 @@
     for t in range(layers):
         for h in range(HALVES):
             for k in range(ys):
-                needed(c, t, h, lambda: own(k, t, h).wait_send())
+                when_needed(c, t, h, lambda: own(k, t, h).wait_send())
             for k in range(1, ys):
                 source = lax.rem(y + ys - k, ys) * 2 + core
-                needed(source, t, h, lambda: relay(k, t, h).wait_send())
+                when_needed(source, t, h, lambda: relay(k, t, h).wait_send())
 
     @pl.when(depth == 0)
     def _():
@@ -404,6 +453,7 @@
             pltpu.VMEM((width, width), BF16),
             pltpu.VMEM((width, width), BF16),
             pltpu.VMEM((width, LANES), F32),
+            pltpu.VMEM((2, width // 2, width // 2), F32),
             dma((ys, layers, HALVES)),
             dma((cols, layers, HALVES)),
             dma((ys, layers, HALVES)),

time: 47.3 us -> 43.9 us (0.928)
  Pallas kernels: 42.8 us -> 39.4 us
    pallas_call x1, Pallas kernels: 42.8 us -> 39.4 us  [on_device(): pl.pallas_call(functools.partial(kernel, rows, cols), out_shape=jax.Shape...]
where the time goes in v3:
time: 43.9 us; the launch traced here: 43.7 us
  Pallas kernels  39.4 us (90%)
  local copies, waits for them, and re-layouts  4.27 us (10%)
    pallas_call x1, Pallas kernels, on_device(): pl.pallas_call(functools.partial(kernel, rows, cols), out_shape=jax.Shape...  39.4 us
    unnamed x7, local copies, waits for them, and re-layouts  4.27 us

profile of v3, /device:TPU:28, one launch (start us, length us, event | category | flops | bytes accessed | tf_op | source)
XLA Modules:
  0.0 43.7 jit_solution(14728081584536570146)
XLA Ops:
  0.0 0.0 copy-start
  0.0 1.2 %copy-done = bf16[2,512,512]{2,1,0:T(8,128)(2,1)S(1)} copy-done((bf16[2,512,512]{2,1,0:T(8,128)(2,1)S(1)}, bf16[2,512,512]{2,1,0:T(8,128)(2,1)}, u32[]{:S(2)}) %copy-start) | copy-done | bytes 1048600
  1.2 0.0 copy-start.1
  1.2 1.0 %copy-done.1 = bf16[2,512,256]{2,1,0:T(8,128)(2,1)S(1)} copy-done((bf16[2,512,256]{2,1,0:T(8,128)(2,1)S(1)}, bf16[2,512,256]{2,1,0:T(8,128)(2,1)}, u32[]{:S(2)}) %copy-start.1) | copy-done | bytes 524312
  2.3 0.0 copy-start.2
  2.3 0.7 %copy-done.2 = f32[256]{0:T(256)S(1)} copy-done((f32[256]{0:T(256)S(1)}, f32[256]{0:T(256)}, u32[]{:S(2)}) %copy-start.2) | copy-done | bytes 1048
  2.9 39.4 %solve_and_update.1 = f32[2,512,512]{2,1,0:T(8,128)S(1)} custom-call(bf16[2,512,512]{2,1,0:T(8,128)(2,1)S(1)} %copy-done, bf16[2,512,256]{2,1,0:T(8,128)(2,1)S(1)} %copy-done.1, f32[1,256]{1,0:T(1,128)S(1)} %bitcast.1), custom_call_target="tpu_custom_call" | custom-call | tf_op jit(solution)/shard_map/solve_and_update/pallas_call | solution.py:441
  42.4 1.3 %copy.5 = f32[2,512,512]{2,1,0:T(8,128)} copy(f32[2,512,512]{2,1,0:T(8,128)S(1)} %solve_and_update.1) | data formatting | bytes 4194304
Async XLA Ops:
  0.0 1.2 %copy-start = (bf16[2,512,512]{2,1,0:T(8,128)(2,1)S(1)}, bf16[2,512,512]{2,1,0:T(8,128)(2,1)}, u32[]{:S(2)}) copy-start(bf16[2,512,512]{2,1,0:T(8,128)(2,1)} %rhs_in.1) | copy-start | bytes 3145732
  1.2 1.0 %copy-start.1 = (bf16[2,512,256]{2,1,0:T(8,128)(2,1)S(1)}, bf16[2,512,256]{2,1,0:T(8,128)(2,1)}, u32[]{:S(2)}) copy-start(bf16[2,512,256]{2,1,0:T(8,128)(2,1)} %panel_in.1) | copy-start | bytes 1572868
  2.3 0.7 %copy-start.2 = (f32[256]{0:T(256)S(1)}, f32[256]{0:T(256)}, u32[]{:S(2)}) copy-start(f32[256]{0:T(256)} %param.5) | copy-start | bytes 3076

commit v4 on v3

--- a/solution.py
+++ b/solution.py
@@ -98,6 +98,9 @@
     line = lax.rem(r, 2)
     depth = r // 2
     depths = rows // 2
+    hub = depths // 2
+    onward = (depth == 0) | ((depth >= hub) & (depth < depths - 1))
+    backward = (depth >= 2) & (depth <= hub)
     layers, width, columns = rhs.shape
     cw = panel_in.shape[2]
     half = cols // 2
@@ -122,15 +125,25 @@
         barrier, inc=1, device_id={"row": depth * 2 + 1 - line}, device_id_type=MESH
     )
 
-    @pl.when(depth > 0)
-    def _():
-        pl.semaphore_signal(barrier, inc=1, device_id={"row": r - 2}, device_id_type=MESH)
-
-    @pl.when(depth < depths - 1)
-    def _():
-        pl.semaphore_signal(barrier, inc=1, device_id={"row": r + 2}, device_id_type=MESH)
-
-    peers = cols + jnp.where(depth > 0, 1, 0) + jnp.where(depth < depths - 1, 1, 0)
+    meets = [
+        (depth == 0, hub),
+        (depth == hub, 0),
+        (depth >= 2, depth - 1),
+        ((depth >= 1) & (depth < depths - 1), depth + 1),
+    ]
+    peers = cols
+    for there, other_depth in meets:
+
+        @pl.when(there)
+        def _():
+            pl.semaphore_signal(
+                barrier,
+                inc=1,
+                device_id={"row": other_depth * 2 + line},
+                device_id_type=MESH,
+            )
+
+        peers = peers + jnp.where(there, 1, 0)
     pl.semaphore_wait(barrier, peers)
 
     def own(k, t, h):
@@ -219,13 +232,14 @@
     def piece(s, n, q):
         return xl.at[s, n, pl.ds(q * piece_rows, piece_rows)]
 
-    def down(s, n, q):
+    def down(way, s, n, q):
+        target = depth - 1 if way else jnp.where(depth == 0, hub, depth + 1)
         return pltpu.make_async_remote_copy(
             src_ref=piece(s, n, q),
             dst_ref=piece(s, n, q),
-            send_sem=z_send.at[n, q],
+            send_sem=z_send.at[way, n, q],
             recv_sem=x_recv.at[s, n, q],
-            device_id={"row": r + 2},
+            device_id={"row": target * 2 + line},
             device_id_type=MESH,
         )
 
@@ -240,11 +254,13 @@
         )
 
     def forward(n, q):
+        for way, there in enumerate((onward, backward)):
+
+            @pl.when(there)
+            def _():
+                down(way, line, n, q).start()
+
         across(line, n, q).start()
-
-        @pl.when(depth < depths - 1)
-        def _():
-            down(line, n, q).start()
 
     def lanes(n):
         return pl.ds(pl.multiple_of(n * LANES, LANES), LANES)
@@ -421,9 +437,11 @@
         for q in range(PIECES):
             across(line, n, q).wait_send()
 
-            @pl.when(depth < depths - 1)
-            def _():
-                down(line, n, q).wait_send()
+            for way, there in enumerate((onward, backward)):
+
+                @pl.when(there)
+                def _():
+                    down(way, line, n, q).wait_send()
 
         leave(n).wait()
 
@@ -459,7 +477,7 @@
             dma((ys, layers, HALVES)),
             dma((cols,)),
             dma((cols,)),
-            dma((chunks, PIECES)),
+            dma((2, chunks, PIECES)),
             dma((chunks, PIECES)),
             dma((2, chunks, PIECES)),
             dma((2,)),

time: 43.9 us -> 43.8 us (level)
  the two profiles are of different devices: /device:TPU:28 before, /device:TPU:12 now
where the time goes in v4:
time: 43.8 us; the launch traced here: 43.5 us
  Pallas kernels  39.3 us (90%)
  local copies, waits for them, and re-layouts  4.27 us (10%)
    pallas_call x1, Pallas kernels, on_device(): pl.pallas_call(functools.partial(kernel, rows, cols), out_shape=jax.Shape...  39.3 us
    unnamed x7, local copies, waits for them, and re-layouts  4.27 us

profile of v4, /device:TPU:12, one launch (start us, length us, event | category | flops | bytes accessed | tf_op | source)
XLA Modules:
  0.0 43.5 jit_solution(3603674558859224326)
XLA Ops:
  0.0 0.0 copy-start
  0.0 1.2 %copy-done = bf16[2,512,512]{2,1,0:T(8,128)(2,1)S(1)} copy-done((bf16[2,512,512]{2,1,0:T(8,128)(2,1)S(1)}, bf16[2,512,512]{2,1,0:T(8,128)(2,1)}, u32[]{:S(2)}) %copy-start) | copy-done | bytes 1048600
  1.2 0.0 copy-start.1
  1.2 1.0 %copy-done.1 = bf16[2,512,256]{2,1,0:T(8,128)(2,1)S(1)} copy-done((bf16[2,512,256]{2,1,0:T(8,128)(2,1)S(1)}, bf16[2,512,256]{2,1,0:T(8,128)(2,1)}, u32[]{:S(2)}) %copy-start.1) | copy-done | bytes 524312
  2.3 0.0 copy-start.2
  2.3 0.7 %copy-done.2 = f32[256]{0:T(256)S(1)} copy-done((f32[256]{0:T(256)S(1)}, f32[256]{0:T(256)}, u32[]{:S(2)}) %copy-start.2) | copy-done | bytes 1048
  2.9 39.3 %solve_and_update.1 = f32[2,512,512]{2,1,0:T(8,128)S(1)} custom-call(bf16[2,512,512]{2,1,0:T(8,128)(2,1)S(1)} %copy-done, bf16[2,512,256]{2,1,0:T(8,128)(2,1)S(1)} %copy-done.1, f32[1,256]{1,0:T(1,128)S(1)} %bitcast.1), custom_call_target="tpu_custom_call" | custom-call | tf_op jit(solution)/shard_map/solve_and_update/pallas_call | solution.py:459
  42.2 1.3 %copy.5 = f32[2,512,512]{2,1,0:T(8,128)} copy(f32[2,512,512]{2,1,0:T(8,128)S(1)} %solve_and_update.1) | data formatting | bytes 4194304
Async XLA Ops:
  0.0 1.2 %copy-start = (bf16[2,512,512]{2,1,0:T(8,128)(2,1)S(1)}, bf16[2,512,512]{2,1,0:T(8,128)(2,1)}, u32[]{:S(2)}) copy-start(bf16[2,512,512]{2,1,0:T(8,128)(2,1)} %rhs_in.1) | copy-start | bytes 3145732
  1.2 1.0 %copy-start.1 = (bf16[2,512,256]{2,1,0:T(8,128)(2,1)S(1)}, bf16[2,512,256]{2,1,0:T(8,128)(2,1)}, u32[]{:S(2)}) copy-start(bf16[2,512,256]{2,1,0:T(8,128)(2,1)} %panel_in.1) | copy-start | bytes 1572868
  2.3 0.7 %copy-start.2 = (f32[256]{0:T(256)S(1)}, f32[256]{0:T(256)}, u32[]{:S(2)}) copy-start(f32[256]{0:T(256)} %param.5) | copy-start | bytes 3076

commit v5 on v4

--- a/solution.py
+++ b/solution.py
@@ -364,6 +364,16 @@
             for q in range(PIECES):
                 forward(n, q)
 
+    early = chunks // 2
+
+    @pl.when(depth > 0)
+    def _():
+        @pl.loop(0, early)
+        def _(n):
+            for q in range(PIECES):
+                across(line, n, q).wait_recv()
+                forward(n, q)
+
     for t in range(1, layers):
         take(t, every)
 
@@ -381,9 +391,12 @@
         def _(n):
             @pl.when(depth > 0)
             def _():
-                for q in range(PIECES):
-                    across(0, n, q).wait_recv()
-                    forward(n, q)
+                @pl.when(n >= early)
+                def _():
+                    for q in range(PIECES):
+                        across(0, n, q).wait_recv()
+                        forward(n, q)
+
                 out[0, :, lanes(n)] = start(0, n) - product(0, 0, n)
 
             for t in range(1, layers):
@@ -408,9 +421,12 @@
         def _(n):
             @pl.when(depth > 0)
             def _():
-                for q in range(PIECES):
-                    across(1, n, q).wait_recv()
-                    forward(n, q)
+                @pl.when(n >= early)
+                def _():
+                    for q in range(PIECES):
+                        across(1, n, q).wait_recv()
+                        forward(n, q)
+
                 for q in range(PIECES):
                     across(0, n, q).wait_recv()
                 out[0, :, lanes(n)] = start(0, n) - product(0, 0, n) - product(1, 0, n)

time: 43.8 us -> 45.8 us (1.046)
  Pallas kernels: 39.3 us -> 41.4 us
    pallas_call x1, Pallas kernels: 39.3 us -> 41.4 us  [on_device(): pl.pallas_call(functools.partial(kernel, rows, cols), out_shape=jax.Shape...]
where the time goes in v5:
time: 45.8 us; the launch traced here: 45.6 us
  Pallas kernels  41.4 us (90%)
  local copies, waits for them, and re-layouts  4.27 us (9%)
    pallas_call x1, Pallas kernels, on_device(): pl.pallas_call(functools.partial(kernel, rows, cols), out_shape=jax.Shape...  41.4 us
    unnamed x7, local copies, waits for them, and re-layouts  4.27 us

profile of v5, /device:TPU:12, one launch (start us, length us, event | category | flops | bytes accessed | tf_op | source)
XLA Modules:
  0.0 45.6 jit_solution(5235269535138373130)
XLA Ops:
  0.0 0.0 copy-start
  0.0 1.2 %copy-done = bf16[2,512,512]{2,1,0:T(8,128)(2,1)S(1)} copy-done((bf16[2,512,512]{2,1,0:T(8,128)(2,1)S(1)}, bf16[2,512,512]{2,1,0:T(8,128)(2,1)}, u32[]{:S(2)}) %copy-start) | copy-done | bytes 1048600
  1.2 0.0 copy-start.1
  1.2 1.0 %copy-done.1 = bf16[2,512,256]{2,1,0:T(8,128)(2,1)S(1)} copy-done((bf16[2,512,256]{2,1,0:T(8,128)(2,1)S(1)}, bf16[2,512,256]{2,1,0:T(8,128)(2,1)}, u32[]{:S(2)}) %copy-start.1) | copy-done | bytes 524312
  2.3 0.0 copy-start.2
  2.3 0.7 %copy-done.2 = f32[256]{0:T(256)S(1)} copy-done((f32[256]{0:T(256)S(1)}, f32[256]{0:T(256)}, u32[]{:S(2)}) %copy-start.2) | copy-done | bytes 1048
  2.9 41.4 %solve_and_update.1 = f32[2,512,512]{2,1,0:T(8,128)S(1)} custom-call(bf16[2,512,512]{2,1,0:T(8,128)(2,1)S(1)} %copy-done, bf16[2,512,256]{2,1,0:T(8,128)(2,1)S(1)} %copy-done.1, f32[1,256]{1,0:T(1,128)S(1)} %bitcast.1), custom_call_target="tpu_custom_call" | custom-call | tf_op jit(solution)/shard_map/solve_and_update/pallas_call | solution.py:475
  44.3 1.3 %copy.5 = f32[2,512,512]{2,1,0:T(8,128)} copy(f32[2,512,512]{2,1,0:T(8,128)S(1)} %solve_and_update.1) | data formatting | bytes 4194304
Async XLA Ops:
  0.0 1.2 %copy-start = (bf16[2,512,512]{2,1,0:T(8,128)(2,1)S(1)}, bf16[2,512,512]{2,1,0:T(8,128)(2,1)}, u32[]{:S(2)}) copy-start(bf16[2,512,512]{2,1,0:T(8,128)(2,1)} %rhs_in.1) | copy-start | bytes 3145732
  1.2 1.0 %copy-start.1 = (bf16[2,512,256]{2,1,0:T(8,128)(2,1)S(1)}, bf16[2,512,256]{2,1,0:T(8,128)(2,1)}, u32[]{:S(2)}) copy-start(bf16[2,512,256]{2,1,0:T(8,128)(2,1)} %panel_in.1) | copy-start | bytes 1572868
  2.3 0.7 %copy-start.2 = (f32[256]{0:T(256)S(1)}, f32[256]{0:T(256)}, u32[]{:S(2)}) copy-start(f32[256]{0:T(256)} %param.5) | copy-start | bytes 3076
